TPU v7x, 32 devices: a whole 2x2x4 slice. The times are simulated.
32 devices in a mesh: dp: 4 (over z), fsdp: 4 (over x, core), tensor: 2 (over y).
Axes of the slice: x: 2, y: 2, z: 4, core: 2. Of those that a mesh axis runs over, the one named last changes fastest.
Arguments:
- tokens: bfloat16 [4096, 8192], P(('dp', 'fsdp'), 'tensor'), may hold values from -700 to 700
- queries: bfloat16 [4096, 8192], P(('dp', 'fsdp'), 'tensor'), may hold values from -140 to 140
- segment_ids: int32 [32, 128], P(('dp', 'fsdp')), may hold values from 0 to 3, never falling along the last dimension, each value on 1 to 64 neighbouring positions
- gain: float32 [8192], P('tensor'), may hold values from 0.1 to 1.9
- key_value_weight: bfloat16 [8192, 2048], P('tensor', 'fsdp'), may hold values from -0.0625 to 0.0625
- plan: int32 [8], replicated, may hold values from 0 to 7, as said below
Outputs:
- attended: bfloat16 [4096, 8192], P(('dp', 'fsdp'), 'tensor')
Inputs may be any that keep to these rules, and one draw needn't show every extreme that they name: plan is a permutation of 0 to 7; from one dp index to another at most 1 micro-batches go, and in every draw some pair of dp indices carries exactly 1.
All inputs are finite; a program needn't handle non-finite values.
Results may differ from a plain program's by a relative error of at most 0.011.
Values may be sent and summed in bfloat16 or wider, within the bound.
A program may use at most 64 MiB of HBM per device.

v0:
```python
import functools

import jax
import jax.numpy as jnp
from jax import lax
from jax.experimental import pallas as pl
from jax.experimental.pallas import tpu as pltpu
from jax.sharding import PartitionSpec as P


HEAD_SIZE = 128


epsilon = 1e-05


def pack_query_kernel(send_ref, query_ref, out_ref):
    out_ref[...] = query_ref[...]


def pack_queries(send_index, queries, length):
    ranks = send_index.shape[0]
    width = queries.shape[1]
    return pl.pallas_call(
        pack_query_kernel,
        grid_spec=pltpu.PrefetchScalarGridSpec(
            num_scalar_prefetch=1,
            grid=(ranks,),
            in_specs=[pl.BlockSpec((length, width), lambda r, send: (send[r], 0))],
            out_specs=pl.BlockSpec((length, width), lambda r, send: (r, 0)),
        ),
        out_shape=jax.ShapeDtypeStruct((ranks * length, width), queries.dtype),
        name="pack_queries",
    )(send_index, queries)


def split_partial_kernel(part_ref, out_ref):
    key = part_ref[:, :HEAD_SIZE]
    high = key.astype(jnp.bfloat16)
    out_ref[:, :HEAD_SIZE] = high
    out_ref[:, HEAD_SIZE : 2 * HEAD_SIZE] = (key - high.astype(jnp.float32)).astype(jnp.bfloat16)
    out_ref[:, 2 * HEAD_SIZE :] = part_ref[:, HEAD_SIZE:].astype(jnp.bfloat16)


def split_partial(partial_value, ranks, spread):
    rows, width = partial_value.shape
    all_heads = width // (2 * HEAD_SIZE)
    heads = all_heads // spread
    height = rows // ranks
    return pl.pallas_call(
        split_partial_kernel,
        grid=(spread, ranks, heads),
        in_specs=[pl.BlockSpec((height, 2 * HEAD_SIZE), lambda b, f, h: (f, b * heads + h))],
        out_specs=pl.BlockSpec(
            (height, 3 * HEAD_SIZE), lambda b, f, h: ((b * ranks + f) * heads + h, 0)
        ),
        out_shape=jax.ShapeDtypeStruct((ranks * all_heads * height, 3 * HEAD_SIZE), jnp.bfloat16),
        name="split_partial",
    )(partial_value)


def pack_kv_kernel(sources, send_ref, slot_ref, *refs):
    *part_refs, document_ref, out_ref = refs
    part_heads = part_refs[0].shape[1]
    heads_kv = part_heads * len(part_refs) // sources
    for h in range(heads_kv):
        first = h // part_heads * sources
        key = value = 0.0
        for part_ref in part_refs[first : first + sources]:
            block = part_ref[0, h % part_heads, 0].astype(jnp.float32)
            key += block[:, :HEAD_SIZE] + block[:, HEAD_SIZE : 2 * HEAD_SIZE]
            value += block[:, 2 * HEAD_SIZE :]
        high = key.astype(jnp.bfloat16)
        low = (key - high.astype(jnp.float32)).astype(jnp.bfloat16)
        for place, part in enumerate((high, low, value.astype(jnp.bfloat16))):
            start = (place * heads_kv + h) * HEAD_SIZE
            out_ref[:, start : start + HEAD_SIZE] = part
    out_ref[:, 3 * heads_kv * HEAD_SIZE :] = document_ref[...]


def pack_kv(send_index, slot_index, parts, documents, sources, length):
    ranks = send_index.shape[0]
    count = slot_index.shape[0]
    rows = documents.shape[0]
    part_heads = parts.shape[0] // (count * rows)
    packed = (3 * part_heads * count // sources + 1) * HEAD_SIZE

    def arrived(w):
        return pl.BlockSpec(
            (1, part_heads, 1, length, 3 * HEAD_SIZE),
            lambda r, send, slot: (slot[w], 0, send[r], 0, 0),
        )

    view = parts.reshape(count, part_heads, rows // length, length, 3 * HEAD_SIZE)
    return pl.pallas_call(
        functools.partial(pack_kv_kernel, sources),
        grid_spec=pltpu.PrefetchScalarGridSpec(
            num_scalar_prefetch=2,
            grid=(ranks,),
            in_specs=[arrived(w) for w in range(count)]
            + [pl.BlockSpec((length, HEAD_SIZE), lambda r, send, slot: (send[r], 0))],
            out_specs=pl.BlockSpec((length, packed), lambda r, send, slot: (r, 0)),
        ),
        out_shape=jax.ShapeDtypeStruct((ranks * length, packed), jnp.bfloat16),
        name="pack_kv",
    )(send_index, slot_index, *[view] * count, documents)


def attend_kernel(
    head_group, keep_ref, query_ref, high_ref, low_ref, value_ref, document_ref, out_ref
):
    length = query_ref.shape[0]
    query = jnp.concatenate(
        [query_ref[:, g * HEAD_SIZE : (g + 1) * HEAD_SIZE] for g in range(head_group)], axis=0
    )
    across = (((1,), (1,)), ((), ()))
    scores = lax.dot_general(query, high_ref[...], across, preferred_element_type=jnp.float32)
    scores += lax.dot_general(query, low_ref[...], across, preferred_element_type=jnp.float32)
    scores = (scores * HEAD_SIZE ** (-0.5)).reshape(head_group, length, length)
    document = document_ref[...].astype(jnp.float32)
    rows = lax.broadcasted_iota(jnp.int32, (length, length), 0)
    columns = lax.broadcasted_iota(jnp.int32, (length, length), 1)
    allowed = (document == document.T) & (columns <= rows)
    scores = jnp.where(allowed[None], scores, -1e30)
    row_max = jnp.max(scores, axis=-1, keepdims=True)
    expo = jnp.exp(scores - row_max)
    weights = (expo / jnp.sum(expo, axis=-1, keepdims=True)).astype(jnp.bfloat16)
    mixed = jnp.dot(
        weights.reshape(head_group * length, length),
        value_ref[...],
        preferred_element_type=jnp.float32,
    ).astype(jnp.bfloat16)
    for g in range(head_group):
        out_ref[:, g * HEAD_SIZE : (g + 1) * HEAD_SIZE] = mixed[g * length : (g + 1) * length]


def attend(keep_index, queries, packed, length):
    batches = keep_index.shape[0]
    heads_kv = (packed.shape[1] // HEAD_SIZE - 1) // 3
    width = queries.shape[1]
    group_width = width // heads_kv

    def part(place):
        return pl.BlockSpec(
            (length, HEAD_SIZE), lambda s, h, keep: (keep[s], place * heads_kv + h)
        )

    return pl.pallas_call(
        functools.partial(attend_kernel, group_width // HEAD_SIZE),
        grid_spec=pltpu.PrefetchScalarGridSpec(
            num_scalar_prefetch=1,
            grid=(batches, heads_kv),
            in_specs=[
                pl.BlockSpec((length, group_width), lambda s, h, keep: (keep[s], h)),
                part(0),
                part(1),
                part(2),
                pl.BlockSpec((length, HEAD_SIZE), lambda s, h, keep: (keep[s], 3 * heads_kv)),
            ],
            out_specs=pl.BlockSpec((length, group_width), lambda s, h, keep: (s, h)),
        ),
        out_shape=jax.ShapeDtypeStruct((batches * length, width), jnp.bfloat16),
        name="attend",
    )(keep_index, queries, packed, packed, packed, packed)


def project(rows, gain, key_value_weight):
    all_rows = lax.all_gather(rows, "fsdp", axis=0, tiled=True)
    values = rows.astype(jnp.float32)
    own_stats = jnp.sum(values * values, axis=1)
    stats = lax.psum(own_stats, "tensor")
    full_width = rows.shape[1] * lax.axis_size("tensor")
    scale = lax.all_gather(lax.rsqrt(stats / full_width + epsilon), "fsdp", axis=0, tiled=True)
    normed = (all_rows.astype(jnp.float32) * scale[:, None] * gain).astype(jnp.bfloat16)
    partial_value = jnp.dot(normed, key_value_weight, preferred_element_type=jnp.float32)
    f_ranks, t_ranks = lax.axis_size("fsdp"), lax.axis_size("tensor")
    joined, spread = max(1, f_ranks // t_ranks), max(1, t_ranks // f_ranks)
    count = f_ranks * spread
    parts = split_partial(partial_value, f_ranks, spread)
    share = parts.shape[0] // count
    f, t = lax.axis_index("fsdp"), lax.axis_index("tensor")
    number = f % joined * t_ranks + t
    arrived = []
    for p in range(count):
        pairs = []
        for i in range(f_ranks):
            for j in range(t_ranks):
                block = (i % joined * t_ranks + j + p) % count
                target = i // joined * spread + block // f_ranks
                pairs.append((i * t_ranks + j, block % f_ranks * t_ranks + target))
        sent = lax.dynamic_slice_in_dim(parts, (number + p) % count * share, share)
        arrived.append(lax.ppermute(sent, ("fsdp", "tensor"), pairs))
    slot_index = (t % spread * f_ranks + f - jnp.arange(count, dtype=jnp.int32)) % count
    return jnp.concatenate(arrived), slot_index


def shards(tokens, queries, segment_ids, gain, key_value_weight, plan):
    rank_count = lax.axis_size("dp")
    own_rank = lax.axis_index("dp")
    batches, length = segment_ids.shape
    own_dest = lax.dynamic_slice_in_dim(plan, own_rank * batches, batches) // batches
    rank_range = jnp.arange(rank_count, dtype=jnp.int32)
    slot_range = jnp.arange(batches, dtype=jnp.int32)
    send_index = jnp.sum(
        jnp.where(own_dest[None, :] == rank_range[:, None], slot_range[None, :], 0), axis=1
    )
    position = jnp.arange(plan.shape[0], dtype=jnp.int32)
    own_slots = own_rank * batches + slot_range
    keep_index = jnp.sum(
        jnp.where(plan[None, :] == own_slots[:, None], position[None, :] // batches, 0), axis=1
    )
    parcels = pack_queries(send_index, queries, length)
    moved_queries = lax.all_to_all(parcels, "dp", split_axis=0, concat_axis=0, tiled=True)
    documents = jnp.broadcast_to(
        segment_ids.reshape(batches * length, 1).astype(jnp.bfloat16),
        (batches * length, HEAD_SIZE),
    )
    parts, slot_index = project(tokens, gain, key_value_weight)
    packed = pack_kv(
        send_index, slot_index, parts, documents, lax.axis_size("tensor"), length
    )
    packed, moved_queries = lax.optimization_barrier((packed, moved_queries))
    moved_kv = lax.all_to_all(packed, "dp", split_axis=0, concat_axis=0, tiled=True)
    return attend(keep_index, moved_queries, moved_kv, length)


def route(plan, ranks, batches, slots, me, step):
    order = list(range(ranks))[::step]
    held = [jnp.int32(-1)] * slots
    transit = [jnp.int32(0)] * slots
    second = [jnp.int32(0)] * slots
    arrived = [jnp.int32(-1)] * slots
    for rank in order:
        here = me == rank
        arrived = [jnp.where(here, held[j], arrived[j]) for j in range(slots)]
        own = [plan[rank * batches + s] for s in range(batches)]
        beyond = lambda place: (step * (place // batches - rank) > 0) & (place >= 0)
        waiting = [beyond(place).astype(jnp.int32) for place in own]
        following = []
        for j in range(slots):
            passes = beyond(held[j]).astype(jnp.int32)
            first_fits = (1 - passes) * waiting[0]
            second_fits = (1 - passes) * (1 - first_fits) * waiting[1]
            waiting = [waiting[0] - first_fits, waiting[1] - second_fits]
            transit[j] = jnp.where(here, passes, transit[j])
            second[j] = jnp.where(here, second_fits, second[j])
            following.append(
                jnp.where(
                    passes > 0,
                    held[j],
                    jnp.where(first_fits > 0, own[0], jnp.where(second_fits > 0, own[1], -1)),
                )
            )
        held = following
    return transit, second, arrived


def pack_parts(part):
    key = part[:, :HEAD_SIZE]
    high = key.astype(jnp.bfloat16)
    low = (key - high.astype(jnp.float32)).astype(jnp.bfloat16)
    return jnp.concatenate([high, low, part[:, HEAD_SIZE:].astype(jnp.bfloat16)], axis=1)


def unpack_parts(packed):
    wide = packed.astype(jnp.float32)
    key = wide[:, :HEAD_SIZE] + wide[:, HEAD_SIZE : 2 * HEAD_SIZE]
    return jnp.concatenate([key, wide[:, 2 * HEAD_SIZE :]], axis=1)


def fused_kernel(
    slots,
    plan_ref,
    tokens_ref,
    query_ref,
    document_ref,
    gain_ref,
    weight_ref,
    out_ref,
    own_rows,
    far_rows,
    weight,
    stats_own,
    stats_far,
    scale_own,
    scale_far,
    query_own,
    query_in,
    query_out,
    documents,
    own_parts,
    far_parts,
    parts_a,
    parts_b,
    kv_own,
    kv_out,
    mixed,
    *rest,
):
    heads = parts_a.shape[0]
    kv_in = rest[:heads]
    (
        load_rows,
        load_weight,
        load_query,
        store_out,
        rows_send,
        rows_recv,
        weight_send,
        weight_recv,
        stats_send,
        stats_recv,
        scale_send,
        scale_recv,
        query_send,
        query_recv,
        document_send,
        document_recv,
        own_send,
        far_send,
        a_recv,
        b_recv,
        kv_send,
        kv_recv,
    ) = rest[heads:]
    ranks = lax.axis_size("dp")
    me, f, t = lax.axis_index("dp"), lax.axis_index("fsdp"), lax.axis_index("tensor")
    batches, length, depth = own_rows.shape
    chunks, _, _, chunk_width = query_own.shape
    core = f % 2
    side = f // 2
    far = f + 2 - 4 * side
    pair = f + 1 - 2 * core
    other = 1 - t
    off = side != t
    away = side == t
    rounds = range(chunks)
    first = jnp.where(2 * me < ranks, 0, 1)
    second_way = 1 - first

    def remote(src, dst, send, recv, device):
        return pltpu.make_async_remote_copy(
            src_ref=src,
            dst_ref=dst,
            send_sem=send,
            recv_sem=recv,
            device_id=device,
            device_id_type=pl.DeviceIdType.MESH,
        )

    rows_local = pltpu.make_async_copy(tokens_ref, own_rows, load_rows)
    rows_local.start()
    query_local = []
    for c in rounds:
        query_local.append(
            pltpu.make_async_copy(
                query_ref.at[:, :, pl.ds(c * chunk_width, chunk_width)],
                query_own.at[c],
                load_query.at[c],
            )
        )
        query_local[c].start()
    weight_local = pltpu.make_async_copy(weight_ref, weight.at[core], load_weight)
    weight_local.start()

    barrier = pltpu.get_barrier_semaphore()
    partners = [(me, far, t), (me, pair, t), (me, f, other), (me, far, other)]
    partners += [((me + k) % ranks, f, t) for k in range(1, ranks)]
    for partner in partners:
        pl.semaphore_signal(
            barrier, inc=1, device_id=partner, device_id_type=pl.DeviceIdType.MESH
        )
    pl.semaphore_wait(barrier, len(partners))

    rows_moves = [
        remote(
            tokens_ref.at[s], far_rows.at[s], rows_send.at[s], rows_recv.at[s], (me, far, t)
        )
        for s in range(batches)
    ]
    for move in rows_moves:
        move.start()
    weight_move = remote(
        weight_ref, weight.at[core], weight_send, weight_recv, (me, pair, t)
    )
    weight_move.start()
    weight_arrives = remote(
        weight_ref, weight.at[1 - core], weight_send, weight_recv, (me, pair, t)
    )

    for s in range(batches):
        line = document_ref[s : s + 1, :].astype(jnp.float32)
        documents[me, s] = jnp.broadcast_to(line, (8, length))

    plan = [plan_ref[i] for i in range(ranks * batches)]
    routes = [route(plan, ranks, batches, slots, me, step) for step in (1, -1)]

    def has_in(way):
        return jnp.where(way == 0, me > 0, me < ranks - 1)

    def has_out(way):
        return jnp.where(way == 0, me < ranks - 1, me > 0)

    def chosen(name, j, way):
        return jnp.where(way == 0, routes[0][name][j], routes[1][name][j])

    def onward(way):
        return (me + 1 - 2 * way, f, t)

    def query_copy(way, c):
        return remote(
            query_out.at[c, way],
            query_in.at[c, way],
            query_send.at[c, way],
            query_recv.at[c, way],
            onward(way),
        )

    def query_step(way, c):
        @pl.when(has_out(way))
        def _():
            @pl.when(has_in(way))
            def _():
                query_copy(way, c).wait_recv()

            for j in range(slots):
                own = jnp.where(
                    chosen(1, j, way) > 0, query_own[c, 1], query_own[c, 0]
                )
                query_out[c, way, j] = jnp.where(
                    chosen(0, j, way) > 0, query_in[c, way, j], own
                )
            query_copy(way, c).start()

    for move in query_local:
        move.wait()
    middle = (me > 0) & (me < ranks - 1)
    ends = (me == 0) | (me == ranks - 1)

    @pl.when(ends)
    def _():
        @pl.loop(0, chunks)
        def _(c):
            query_step(first, c)

    def query_round(c):
        @pl.when(middle)
        def _():
            query_step(first, c)
            if c:
                query_step(second_way, c - 1)
            if c == chunks - 1:
                query_step(second_way, c)

    document_moves = [
        remote(
            documents.at[me],
            documents.at[me],
            document_send.at[k - 1],
            document_recv.at[k - 1],
            ((me + k) % ranks, f, t),
        )
        for k in range(1, ranks)
    ]
    document_arrivals = [
        remote(
            documents.at[(me + ranks - k) % ranks],
            documents.at[(me + ranks - k) % ranks],
            document_send.at[k - 1],
            document_recv.at[k - 1],
            ((me + k) % ranks, f, t),
        )
        for k in range(1, ranks)
    ]
    for move in document_moves:
        move.start()

    rows_of = lax.broadcasted_iota(jnp.int32, (length, length), 0)
    columns_of = lax.broadcasted_iota(jnp.int32, (length, length), 1)
    diagonal = rows_of == columns_of
    block = 4 * HEAD_SIZE
    blocks = depth // block

    rows_local.wait()
    for s in range(batches):

        def squares(i, total, s=s):
            start = pl.multiple_of(i * block, block)
            values = own_rows[s, :, pl.ds(start, block)].astype(jnp.float32)
            values = values * values
            for g in range(block // HEAD_SIZE):
                total += values[:, g * HEAD_SIZE : (g + 1) * HEAD_SIZE]
            return total

        total = lax.fori_loop(
            0, blocks, squares, jnp.zeros((length, HEAD_SIZE), jnp.float32)
        )
        column = jnp.sum(total, axis=1, keepdims=True)
        line = jnp.sum(jnp.where(diagonal, column, 0.0), axis=0, keepdims=True)
        stats_own[s] = jnp.broadcast_to(line, (8, length))
    stats_move = remote(stats_own, stats_far, stats_send, stats_recv, (me, f, other))
    stats_move.start()
    stats_move.wait_recv()
    full_width = depth * lax.axis_size("tensor")
    scale_own[...] = lax.rsqrt((stats_own[...] + stats_far[...]) / full_width + epsilon)
    scale_move = remote(scale_own, scale_far, scale_send, scale_recv, (me, far, t))
    scale_move.start()

    def normalize(rows, scale, s):
        line = jnp.broadcast_to(scale[s, 0:1, :], (length, length))
        column = jnp.sum(jnp.where(diagonal, line, 0.0), axis=1, keepdims=True)

        @pl.loop(0, blocks)
        def _(i):
            start = pl.multiple_of(i * block, block)
            values = rows[s, :, pl.ds(start, block)].astype(jnp.float32)
            values = values * column * gain_ref[:, pl.ds(start, block)]
            rows[s, :, pl.ds(start, block)] = values.astype(jnp.bfloat16)

    for s in range(batches):
        normalize(own_rows, scale_own, s)

    def multiply(rows, h):
        half = heads // 2
        start = pl.multiple_of((h % half) * 2 * HEAD_SIZE, 2 * HEAD_SIZE)
        part = jnp.dot(
            rows[...].reshape(batches * length, depth),
            weight[h // half, :, pl.ds(start, 2 * HEAD_SIZE)],
            preferred_element_type=jnp.float32,
        )
        return pack_parts(part).reshape(batches, length, 3 * HEAD_SIZE)

    def own_copy(h):
        return remote(
            own_parts.at[h], parts_b.at[h], own_send.at[h], b_recv.at[h], (me, f, other)
        )

    def far_copy_a(h):
        return remote(
            far_parts.at[h], parts_a.at[h], far_send.at[h], a_recv.at[h], (me, far, t)
        )

    def far_copy_b(h):
        return remote(
            far_parts.at[h], parts_b.at[h], far_send.at[h], b_recv.at[h], (me, far, other)
        )

    def own_head(h):
        packed = multiply(own_rows, h)

        @pl.when(off)
        def _():
            own_parts[h] = packed
            own_copy(h).start()

        @pl.when(away)
        def _():
            parts_a[h] = packed

    def far_head(h):
        far_parts[h] = multiply(far_rows, h)

        @pl.when(off)
        def _():
            far_copy_b(h).start()

        @pl.when(away)
        def _():
            far_copy_a(h).start()

    query_round(0)
    weight_local.wait()
    weight_arrives.wait_recv()
    pl.loop(0, heads // 2)(own_head)
    query_round(1)
    pl.loop(heads // 2, heads)(own_head)

    def take_rows(s):
        rows_moves[s].wait_recv()
        if s == 0:
            scale_move.wait_recv()
        normalize(far_rows, scale_far, s)

    marks = [max(1, chunks // slots - 1), max(1, 2 * chunks // slots - 1)]
    for c in range(1, chunks):
        if c > 1:
            query_round(c)
        for s in range(batches):
            if marks[s] == c:
                take_rows(s)
        if marks[-1] == c:
            pl.loop(0, heads)(far_head)

    def kv_copy(way, h):
        return remote(
            kv_out.at[h, way],
            kv_in[h].at[way],
            kv_send.at[h, way],
            kv_recv.at[h, way],
            onward(way),
        )

    def kv_step(way, h):
        @pl.when(has_out(way))
        def _():
            @pl.when(has_in(way))
            def _():
                kv_copy(way, h).wait_recv()

            for j in range(slots):
                own = jnp.where(chosen(1, j, way) > 0, kv_own[h, 1], kv_own[h, 0])
                kv_out[h, way, j] = jnp.where(
                    chosen(0, j, way) > 0, kv_in[h][way, j], own
                )
            kv_copy(way, h).start()

    def join(h):
        @pl.when(off)
        def _():
            far_copy_a(h).wait_recv()

        far_copy_b(h).wait_recv()
        for s in range(batches):
            kv_own[h, s] = pack_parts(
                unpack_parts(parts_a[h, s]) + unpack_parts(parts_b[h, s])
            )

    per_head = chunks // heads
    group = per_head * chunk_width // HEAD_SIZE
    across = (((1,), (1,)), ((), ()))

    def place_of(s):
        want = me * batches + s
        own_at = jnp.int32(-1)
        for b in range(batches):
            for rank in range(ranks):
                hit = (me == rank) & (plan[rank * batches + b] == want)
                own_at = jnp.where(hit, b, own_at)
        in_at = []
        for way in range(2):
            at = jnp.int32(-1)
            for j in range(slots):
                at = jnp.where(routes[way][2][j] == want, j, at)
            in_at.append(at)
        source = jnp.int32(0)
        for b in range(ranks * batches):
            source = jnp.where(plan[b] == want, b, source)
        return own_at, in_at[0], in_at[1], source

    def pick(own, coming, places):
        own_at, right_at, left_at, _ = places
        value = jnp.where(
            right_at >= 0, coming(0, jnp.maximum(right_at, 0)), own(jnp.maximum(own_at, 0))
        )
        return jnp.where(left_at >= 0, coming(1, jnp.maximum(left_at, 0)), value)

    def out_copy(s, h):
        wide = group * HEAD_SIZE
        return pltpu.make_async_copy(
            mixed.at[s, h],
            out_ref.at[pl.ds(s * length, length), pl.ds(h * wide, wide)],
            store_out.at[s, h],
        )

    spots = [place_of(s) for s in range(batches)]

    def settle(copy, index):
        for way in range(2):

            @pl.when(has_in(way) & jnp.logical_not(has_out(way)))
            def _():
                copy(way, index).wait_recv()

    def attend_head(h):
        settle(kv_copy, h)

        @pl.loop(0, batches)
        def _(s):
            places = [jnp.where(s == 0, a, b) for a, b in zip(*spots)]
            tiles = []
            for c in range(h * per_head, (h + 1) * per_head):
                wide = pick(
                    lambda at: query_own[c, at], lambda way, at: query_in[c, way, at], places
                )
                for g in range(chunk_width // HEAD_SIZE):
                    tiles.append(wide[:, g * HEAD_SIZE : (g + 1) * HEAD_SIZE])
            query = jnp.concatenate(tiles, axis=0)
            kv = pick(lambda at: kv_own[h, at], lambda way, at: kv_in[h][way, at], places)
            high, low, value = (
                kv[:, i * HEAD_SIZE : (i + 1) * HEAD_SIZE] for i in range(3)
            )
            line = documents[places[3] // batches, places[3] % batches]
            line = jnp.broadcast_to(line[0:1, :], (length, length))
            scores = lax.dot_general(query, high, across, preferred_element_type=jnp.float32)
            scores += lax.dot_general(query, low, across, preferred_element_type=jnp.float32)
            scores = (scores * HEAD_SIZE ** (-0.5)).reshape(group, length, length)
            allowed = (line == line.T) & (columns_of <= rows_of)
            scores = jnp.where(allowed[None], scores, -1e30)
            row_max = jnp.max(scores, axis=-1, keepdims=True)
            expo = jnp.exp(scores - row_max)
            weights = (expo / jnp.sum(expo, axis=-1, keepdims=True)).astype(jnp.bfloat16)
            result = jnp.dot(
                weights.reshape(group * length, length),
                value,
                preferred_element_type=jnp.float32,
            ).astype(jnp.bfloat16)
            for g in range(group):
                mixed[s, h, :, g * HEAD_SIZE : (g + 1) * HEAD_SIZE] = result[
                    g * length : (g + 1) * length
                ]
            out_copy(s, h).start()

    for step in range(heads + 2):
        if step < heads:
            join(step)
            kv_step(first, step)
        if 1 <= step <= heads:
            kv_step(second_way, step - 1)
        if step == 1:
            for c in rounds:
                settle(query_copy, c)
            for move in document_arrivals:
                move.wait_recv()
        if step >= 2:
            attend_head(step - 2)

    for move in rows_moves + [weight_move, stats_move, scale_move] + document_moves:
        move.wait_send()
    for way in range(2):

        @pl.when(has_out(way))
        def _():
            for c in rounds:
                query_copy(way, c).wait_send()
            for h in range(heads):
                kv_copy(way, h).wait_send()

    for h in range(heads):

        @pl.when(off)
        def _():
            own_copy(h).wait_send()

        far_copy_a(h).wait_send()
        for s in range(batches):
            out_copy(s, h).wait()


def fused(slots, plan, tokens, queries, segment_ids, gain, key_value_weight):
    ranks = lax.axis_size("dp")
    batches, length = segment_ids.shape
    rows, depth = tokens.shape
    width = queries.shape[1]
    heads = 2 * key_value_weight.shape[1] // (2 * HEAD_SIZE)
    chunks = 2 * heads
    chunk_width = width // chunks
    packed = 3 * HEAD_SIZE
    bf16, f32 = jnp.bfloat16, jnp.float32
    dma = pltpu.SemaphoreType.DMA
    anywhere = pl.BlockSpec(memory_space=pl.ANY)
    return pl.pallas_call(
        functools.partial(fused_kernel, slots),
        out_shape=jax.ShapeDtypeStruct((rows, width), bf16),
        in_specs=[
            pl.BlockSpec(memory_space=pltpu.SMEM),
            anywhere,
            anywhere,
            pl.BlockSpec(memory_space=pltpu.VMEM),
            pl.BlockSpec(memory_space=pltpu.VMEM),
            anywhere,
        ],
        out_specs=anywhere,
        scratch_shapes=[
            pltpu.VMEM((batches, length, depth), bf16),
            pltpu.VMEM((batches, length, depth), bf16),
            pltpu.VMEM((2, depth, key_value_weight.shape[1]), bf16),
            pltpu.VMEM((batches, 8, length), f32),
            pltpu.VMEM((batches, 8, length), f32),
            pltpu.VMEM((batches, 8, length), f32),
            pltpu.VMEM((batches, 8, length), f32),
            pltpu.VMEM((chunks, batches, length, chunk_width), bf16),
            pltpu.VMEM((chunks, 2, slots, length, chunk_width), bf16),
            pltpu.VMEM((chunks, 2, slots, length, chunk_width), bf16),
            pltpu.VMEM((ranks, batches, 8, length), f32),
            pltpu.VMEM((heads, batches, length, packed), bf16),
            pltpu.VMEM((heads, batches, length, packed), bf16),
            pltpu.VMEM((heads, batches, length, packed), bf16),
            pltpu.VMEM((heads, batches, length, packed), bf16),
            pltpu.VMEM((heads, batches, length, packed), bf16),
            pltpu.VMEM((heads, 2, slots, length, packed), bf16),
            pltpu.VMEM((batches, heads, length, width // heads), bf16),
        ]
        + [pltpu.VMEM((2, slots, length, packed), bf16)] * heads
        + [
            dma,
            dma,
            dma((chunks,)),
            dma((batches, heads)),
            dma((batches,)),
            dma((batches,)),
            dma,
            dma,
            dma,
            dma,
            dma,
            dma,
            dma((chunks, 2)),
            dma((chunks, 2)),
            dma((ranks - 1,)),
            dma((ranks - 1,)),
            dma((heads,)),
            dma((heads,)),
            dma((heads,)),
            dma((heads,)),
            dma((heads, 2)),
            dma((heads, 2)),
        ],
        compiler_params=pltpu.CompilerParams(
            collective_id=slots, has_side_effects=True, vmem_limit_bytes=62 * 2**20
        ),
        name="fused",
    )(
        plan,
        tokens.reshape(batches, length, depth),
        queries.reshape(batches, length, width),
        segment_ids,
        gain.reshape(1, depth),
        key_value_weight,
    )


def fused_shards(tokens, queries, segment_ids, gain, key_value_weight, plan):
    batches = segment_ids.shape[0]
    most = batches * (lax.axis_size("dp") // 2)
    return fused(most, plan, tokens, queries, segment_ids, gain, key_value_weight)


def solution(mesh):
    placed = (
        P(("dp", "fsdp"), "tensor"),
        P(("dp", "fsdp"), "tensor"),
        P(("dp", "fsdp"), None),
        P("tensor"),
        P("tensor", "fsdp"),
        P(),
    )
    small = mesh.shape["tensor"] == 2 and mesh.shape["fsdp"] == 4 and mesh.shape["dp"] <= 4
    return jax.shard_map(
        fused_shards if small else shards,
        mesh=mesh,
        in_specs=placed,
        out_specs=P(("dp", "fsdp"), "tensor"),
        check_vma=False,
    )
```

profile of v0, /device:TPU:0, one launch (start us, length us, event | category | flops | bytes accessed | tf_op | source)
XLA Modules:
  0.0 173.6 jit_solution(15547077674085859077)
XLA Ops:
  0.0 170.4 %fused.1 = bf16[256,4096]{1,0:T(8,128)(2,1)} custom-call(s32[8]{0:T(128)} %plan_ref.1, bf16[2,128,4096]{2,1,0:T(8,128)(2,1)} %bitcast.3, bf16[2,128,4096]{2,1,0:T(8,128)(2,1)} %bitcast.4, s32[2,128]{1,0:T(2,128)} %document_ref.1, f32[1,4096]{1,0:T(1,128)} %bitcast.5, bf16[4096,512]{1,0:T(8,128)(2,1)} %weight_ref.1), custom_call_target="tpu_custom_call" | custom-call | tf_op jit(solution)/shard_map/fused/pallas_call | solution.py:761
  170.4 3.1 %copy.8 = bf16[256,4096]{1,0:T(8,128)(2,1)} copy(bf16[256,4096]{1,0:T(8,128)(2,1)} %fused.1) | data formatting | bytes 4194304
where the time goes:
time: 174 us
  Pallas kernels  170 us (98%)
  local copies, waits for them, and re-layouts  3.13 us (2%)
    pallas_call x1, Pallas kernels, fused(): pl.pallas_call(functools.partial(fused_kernel, slots), out_shape=jax.Shap...  170 us

commit v1 on v0

--- a/solution.py
+++ b/solution.py
@@ -830,9 +830,18 @@
 
 
 def fused_shards(tokens, queries, segment_ids, gain, key_value_weight, plan):
+    ranks = lax.axis_size("dp")
     batches = segment_ids.shape[0]
-    most = batches * (lax.axis_size("dp") // 2)
-    return fused(most, plan, tokens, queries, segment_ids, gain, key_value_weight)
+    target = plan // batches
+    source = jnp.arange(plan.shape[0], dtype=jnp.int32) // batches
+    cuts = jnp.arange(1, ranks, dtype=jnp.int32)[:, None]
+    crossing = jnp.sum((source < cuts) & (target >= cuts), axis=1)
+    most = batches * (ranks // 2)
+    branches = [functools.partial(fused, slots) for slots in range(batches, most + 1)]
+    index = jnp.clip(jnp.max(crossing) - batches, 0, most - batches)
+    return lax.switch(
+        index, branches, plan, tokens, queries, segment_ids, gain, key_value_weight
+    )
 
 
 def solution(mesh):

time: 174 us -> 119 us (0.68)
  Pallas kernels: 170 us -> 112 us
    pallas_call x1, Pallas kernels: 170 us -> 112 us  [fused(): pl.pallas_call(functools.partial(fused_kernel, slots), out_shape=jax.Shap...]
where the time goes in v1:
time: 119 us; the launch traced here: 117 us
  Pallas kernels  112 us (94%)
  local copies, waits for them, and re-layouts  3.13 us (3%)
  other arithmetic  1.48 us (1%)
    pallas_call x1, Pallas kernels, fused(): pl.pallas_call(functools.partial(fused_kernel, slots), out_shape=jax.Shap...  112 us
    unnamed x1, local copies, waits for them, and re-layouts  3.13 us

profile of v1, /device:TPU:0, one launch (start us, length us, event | category | flops | bytes accessed | tf_op | source)
XLA Modules:
  0.0 117.4 jit_solution(14937969498579099611)
XLA Ops:
  0.0 0.7 and_select_fusion
  0.7 0.2 convert_reduce_fusion
  0.8 0.6 reduce_max.9
  2.1 112.1 %conditional.1 = (bf16[256,4096]{1,0:T(8,128)(2,1)}) conditional(s32[]{:T(128)} %clamp.3, (bf16[256,4096]{1,0:T(8,128)(2,1)}, bf16[256,4096]{1,0:T(8,128)(2,1)}, f32[4096]{0:T(1024)}, s32[8]{0:T(128)}, s32[2,128]{1,0:T(2,128)}, /*index=5*/bf16[4096,512]{1,0:T(8,128)(2,1)}) %tuple.14, (bf16[256,4096]{1,0:T(8,128)(2,1)}, ...), branch_computations={%region_2.3_spmd, %region_3.4_spmd, %region_4.5_spmd} | conditional | bytes 8 | solution.py:842
  2.2 111.9 %fused.3 = bf16[256,4096]{1,0:T(8,128)(2,1)} custom-call(s32[8]{0:T(128)} %get-tuple-element.44.plan_ref, bf16[2,128,4096]{2,1,0:T(8,128)(2,1)} %bitcast.9, bf16[2,128,4096]{2,1,0:T(8,128)(2,1)} %bitcast.12, s32[2,128]{1,0:T(2,128)} %get-tuple-element.48.document_ref, f32[1,4096]{1,0:T(1,128)} %bitcast.15, bf16[4096,512]{1,0:T(8,128)(2,1)} %get-tuple-element.50.weight_ref), custom_call_target="tpu_custom_call" | custom-call | tf_op jit(solution)/shard_map/cond/branch_0_fun/fused/pallas_call | solution.py:761
  114.3 3.1 %copy.14 = bf16[256,4096]{1,0:T(8,128)(2,1)} copy(bf16[256,4096]{1,0:T(8,128)(2,1)} %get-tuple-element.63) | data formatting | bytes 4194304
  (1 shorter events, 0.0 us)

commit v2 on v1

--- a/solution.py
+++ b/solution.py
@@ -2,6 +2,7 @@
 
 import jax
 import jax.numpy as jnp
+import numpy as np
 from jax import lax
 from jax.experimental import pallas as pl
 from jax.experimental.pallas import tpu as pltpu
@@ -297,8 +298,8 @@
     mixed,
     *rest,
 ):
-    heads = parts_a.shape[0]
-    kv_in = rest[:heads]
+    pieces = parts_a.shape[0]
+    kv_in = rest[:pieces]
     (
         load_rows,
         load_weight,
@@ -322,10 +323,15 @@
         b_recv,
         kv_send,
         kv_recv,
-    ) = rest[heads:]
+    ) = rest[pieces:]
     ranks = lax.axis_size("dp")
     me, f, t = lax.axis_index("dp"), lax.axis_index("fsdp"), lax.axis_index("tensor")
     batches, length, depth = own_rows.shape
+    heads = mixed.shape[1]
+    height = parts_a.shape[2]
+    per_piece = pieces // heads
+    tall = length // 4
+    strips = batches * length // tall
     chunks, _, _, chunk_width = query_own.shape
     core = f % 2
     side = f // 2
@@ -335,6 +341,7 @@
     off = side != t
     away = side == t
     rounds = range(chunks)
+    ahead = 2
     first = jnp.where(2 * me < ranks, 0, 1)
     second_way = 1 - first
 
@@ -372,13 +379,20 @@
         )
     pl.semaphore_wait(barrier, len(partners))
 
-    rows_moves = [
-        remote(
-            tokens_ref.at[s], far_rows.at[s], rows_send.at[s], rows_recv.at[s], (me, far, t)
-        )
-        for s in range(batches)
-    ]
-    for move in rows_moves:
+    rows_moves = []
+    for q in range(strips):
+        part = (q * tall // length, pl.ds(q * tall % length, tall))
+        rows_moves.append(
+            remote(
+                tokens_ref.at[part],
+                far_rows.at[part],
+                rows_send.at[q],
+                rows_recv.at[q],
+                (me, far, t),
+            )
+        )
+
+    for move in rows_moves[:ahead]:
         move.start()
     weight_move = remote(
         weight_ref, weight.at[core], weight_send, weight_recv, (me, pair, t)
@@ -391,66 +405,6 @@
     for s in range(batches):
         line = document_ref[s : s + 1, :].astype(jnp.float32)
         documents[me, s] = jnp.broadcast_to(line, (8, length))
-
-    plan = [plan_ref[i] for i in range(ranks * batches)]
-    routes = [route(plan, ranks, batches, slots, me, step) for step in (1, -1)]
-
-    def has_in(way):
-        return jnp.where(way == 0, me > 0, me < ranks - 1)
-
-    def has_out(way):
-        return jnp.where(way == 0, me < ranks - 1, me > 0)
-
-    def chosen(name, j, way):
-        return jnp.where(way == 0, routes[0][name][j], routes[1][name][j])
-
-    def onward(way):
-        return (me + 1 - 2 * way, f, t)
-
-    def query_copy(way, c):
-        return remote(
-            query_out.at[c, way],
-            query_in.at[c, way],
-            query_send.at[c, way],
-            query_recv.at[c, way],
-            onward(way),
-        )
-
-    def query_step(way, c):
-        @pl.when(has_out(way))
-        def _():
-            @pl.when(has_in(way))
-            def _():
-                query_copy(way, c).wait_recv()
-
-            for j in range(slots):
-                own = jnp.where(
-                    chosen(1, j, way) > 0, query_own[c, 1], query_own[c, 0]
-                )
-                query_out[c, way, j] = jnp.where(
-                    chosen(0, j, way) > 0, query_in[c, way, j], own
-                )
-            query_copy(way, c).start()
-
-    for move in query_local:
-        move.wait()
-    middle = (me > 0) & (me < ranks - 1)
-    ends = (me == 0) | (me == ranks - 1)
-
-    @pl.when(ends)
-    def _():
-        @pl.loop(0, chunks)
-        def _(c):
-            query_step(first, c)
-
-    def query_round(c):
-        @pl.when(middle)
-        def _():
-            query_step(first, c)
-            if c:
-                query_step(second_way, c - 1)
-            if c == chunks - 1:
-                query_step(second_way, c)
 
     document_moves = [
         remote(
@@ -474,6 +428,65 @@
     ]
     for move in document_moves:
         move.start()
+
+    plan = [plan_ref[i] for i in range(ranks * batches)]
+    routes = [route(plan, ranks, batches, slots, me, step) for step in (1, -1)]
+
+    def has_in(way):
+        return jnp.where(way == 0, me > 0, me < ranks - 1)
+
+    def has_out(way):
+        return jnp.where(way == 0, me < ranks - 1, me > 0)
+
+    def chosen(name, j, way):
+        return jnp.where(way == 0, routes[0][name][j], routes[1][name][j])
+
+    def onward(way):
+        return (me + 1 - 2 * way, f, t)
+
+    def query_copy(way, c):
+        return remote(
+            query_out.at[c, way],
+            query_in.at[c, way],
+            query_send.at[c, way],
+            query_recv.at[c, way],
+            onward(way),
+        )
+
+    def query_step(way, c):
+        @pl.when(has_out(way))
+        def _():
+            @pl.when(has_in(way))
+            def _():
+                query_copy(way, c).wait_recv()
+
+            for j in range(slots):
+                own = jnp.where(
+                    chosen(1, j, way) > 0, query_own[c, 1], query_own[c, 0]
+                )
+                query_out[c, way, j] = jnp.where(
+                    chosen(0, j, way) > 0, query_in[c, way, j], own
+                )
+            query_copy(way, c).start()
+
+    for move in query_local:
+        move.wait()
+    middle = (me > 0) & (me < ranks - 1)
+    ends = (me == 0) | (me == ranks - 1)
+
+    @pl.when(ends)
+    def _():
+        @pl.loop(0, chunks)
+        def _(c):
+            query_step(first, c)
+
+    def query_round(c):
+        @pl.when(middle)
+        def _():
+            if c < chunks:
+                query_step(first, c)
+            if c:
+                query_step(second_way, c - 1)
 
     rows_of = lax.broadcasted_iota(jnp.int32, (length, length), 0)
     columns_of = lax.broadcasted_iota(jnp.int32, (length, length), 1)
@@ -505,20 +518,23 @@
     scale_own[...] = lax.rsqrt((stats_own[...] + stats_far[...]) / full_width + epsilon)
     scale_move = remote(scale_own, scale_far, scale_send, scale_recv, (me, far, t))
     scale_move.start()
-
-    def normalize(rows, scale, s):
+    for move in rows_moves[ahead:]:
+        move.start()
+
+    def normalize(rows, scale, s, top, count):
         line = jnp.broadcast_to(scale[s, 0:1, :], (length, length))
         column = jnp.sum(jnp.where(diagonal, line, 0.0), axis=1, keepdims=True)
+        column = column[top : top + count]
 
         @pl.loop(0, blocks)
         def _(i):
             start = pl.multiple_of(i * block, block)
-            values = rows[s, :, pl.ds(start, block)].astype(jnp.float32)
+            values = rows[s, top : top + count, pl.ds(start, block)].astype(jnp.float32)
             values = values * column * gain_ref[:, pl.ds(start, block)]
-            rows[s, :, pl.ds(start, block)] = values.astype(jnp.bfloat16)
+            rows[s, top : top + count, pl.ds(start, block)] = values.astype(jnp.bfloat16)
 
     for s in range(batches):
-        normalize(own_rows, scale_own, s)
+        normalize(own_rows, scale_own, s, 0, length)
 
     def multiply(rows, h):
         half = heads // 2
@@ -530,66 +546,76 @@
         )
         return pack_parts(part).reshape(batches, length, 3 * HEAD_SIZE)
 
-    def own_copy(h):
+    def own_copy(i):
         return remote(
-            own_parts.at[h], parts_b.at[h], own_send.at[h], b_recv.at[h], (me, f, other)
-        )
-
-    def far_copy_a(h):
+            own_parts.at[i], parts_b.at[i], own_send.at[i], b_recv.at[i], (me, f, other)
+        )
+
+    def far_copy_a(i):
         return remote(
-            far_parts.at[h], parts_a.at[h], far_send.at[h], a_recv.at[h], (me, far, t)
-        )
-
-    def far_copy_b(h):
+            far_parts.at[i], parts_a.at[i], far_send.at[i], a_recv.at[i], (me, far, t)
+        )
+
+    def far_copy_b(i):
         return remote(
-            far_parts.at[h], parts_b.at[h], far_send.at[h], b_recv.at[h], (me, far, other)
+            far_parts.at[i], parts_b.at[i], far_send.at[i], b_recv.at[i], (me, far, other)
         )
 
     def own_head(h):
         packed = multiply(own_rows, h)
+        for j in range(per_piece):
+            i = h * per_piece + j
+            piece = packed[:, j * height : (j + 1) * height]
+
+            @pl.when(off)
+            def _():
+                own_parts[i] = piece
+                own_copy(i).start()
+
+            @pl.when(away)
+            def _():
+                parts_a[i] = piece
+
+    def far_head(h):
+        packed = multiply(far_rows, h)
+        for j in range(per_piece):
+            far_parts[h * per_piece + j] = packed[:, j * height : (j + 1) * height]
+
+    def send_far(i):
+        if i % per_piece == 0:
+            far_head(i // per_piece)
 
         @pl.when(off)
         def _():
-            own_parts[h] = packed
-            own_copy(h).start()
+            far_copy_b(i).start()
 
         @pl.when(away)
         def _():
-            parts_a[h] = packed
-
-    def far_head(h):
-        far_parts[h] = multiply(far_rows, h)
-
-        @pl.when(off)
-        def _():
-            far_copy_b(h).start()
-
-        @pl.when(away)
-        def _():
-            far_copy_a(h).start()
-
-    query_round(0)
-    weight_local.wait()
-    weight_arrives.wait_recv()
-    pl.loop(0, heads // 2)(own_head)
-    query_round(1)
-    pl.loop(heads // 2, heads)(own_head)
-
-    def take_rows(s):
-        rows_moves[s].wait_recv()
-        if s == 0:
+            far_copy_a(i).start()
+
+    def take_rows(q):
+        rows_moves[q].wait_recv()
+        if q == 0:
             scale_move.wait_recv()
-        normalize(far_rows, scale_far, s)
-
-    marks = [max(1, chunks // slots - 1), max(1, 2 * chunks // slots - 1)]
-    for c in range(1, chunks):
-        if c > 1:
-            query_round(c)
-        for s in range(batches):
-            if marks[s] == c:
-                take_rows(s)
-        if marks[-1] == c:
-            pl.loop(0, heads)(far_head)
+        normalize(far_rows, scale_far, q * tall // length, q * tall % length, tall)
+
+    taken = 0
+    later = list(range(chunks + 1))
+    while taken < strips:
+        c = later.pop(0)
+        query_round(c)
+        paced = (c + 1) * slots * length * chunk_width // (tall * depth)
+        if c == 0:
+            weight_local.wait()
+            weight_arrives.wait_recv()
+        if c < 2:
+            pl.loop(c * heads // 2, (c + 1) * heads // 2)(own_head)
+        upto = paced
+        if (c + 2) * slots * length * chunk_width >= strips * tall * depth:
+            upto = strips
+        while taken < upto:
+            take_rows(taken)
+            taken += 1
 
     def kv_copy(way, h):
         return remote(
@@ -672,7 +698,8 @@
                 copy(way, index).wait_recv()
 
     def attend_head(h):
-        settle(kv_copy, h)
+        for i in range(h * per_piece, (h + 1) * per_piece):
+            settle(kv_copy, i)
 
         @pl.loop(0, batches)
         def _(s):
@@ -685,7 +712,13 @@
                 for g in range(chunk_width // HEAD_SIZE):
                     tiles.append(wide[:, g * HEAD_SIZE : (g + 1) * HEAD_SIZE])
             query = jnp.concatenate(tiles, axis=0)
-            kv = pick(lambda at: kv_own[h, at], lambda way, at: kv_in[h][way, at], places)
+            kv = jnp.concatenate(
+                [
+                    pick(lambda at: kv_own[i, at], lambda way, at: kv_in[i][way, at], places)
+                    for i in range(h * per_piece, (h + 1) * per_piece)
+                ],
+                axis=0,
+            )
             high, low, value = (
                 kv[:, i * HEAD_SIZE : (i + 1) * HEAD_SIZE] for i in range(3)
             )
@@ -710,19 +743,29 @@
                 ]
             out_copy(s, h).start()
 
-    for step in range(heads + 2):
-        if step < heads:
+    for i in range(pieces):
+        send_far(i)
+        if i == per_piece - 1 and len(later) > 1:
+            query_round(later.pop(0))
+    while len(later) > 1:
+        query_round(later.pop(0))
+    for step in range(pieces + 1):
+        if step < pieces:
             join(step)
             kv_step(first, step)
-        if 1 <= step <= heads:
-            kv_step(second_way, step - 1)
         if step == 1:
+            query_round(later.pop(0))
             for c in rounds:
                 settle(query_copy, c)
             for move in document_arrivals:
                 move.wait_recv()
         if step >= 2:
-            attend_head(step - 2)
+            kv_step(second_way, step - 2)
+        if step == pieces:
+            kv_step(second_way, step - 1)
+        if step == pieces:
+            for h in range(heads):
+                attend_head(h)
 
     for move in rows_moves + [weight_move, stats_move, scale_move] + document_moves:
         move.wait_send()
@@ -732,16 +775,17 @@
         def _():
             for c in rounds:
                 query_copy(way, c).wait_send()
-            for h in range(heads):
-                kv_copy(way, h).wait_send()
-
-    for h in range(heads):
+            for i in range(pieces):
+                kv_copy(way, i).wait_send()
+
+    for i in range(pieces):
 
         @pl.when(off)
         def _():
-            own_copy(h).wait_send()
-
-        far_copy_a(h).wait_send()
+            own_copy(i).wait_send()
+
+        far_copy_a(i).wait_send()
+    for h in range(heads):
         for s in range(batches):
             out_copy(s, h).wait()
 
@@ -754,7 +798,8 @@
     heads = 2 * key_value_weight.shape[1] // (2 * HEAD_SIZE)
     chunks = 2 * heads
     chunk_width = width // chunks
-    packed = 3 * HEAD_SIZE
+    pieces = 2 * heads
+    packed = (length // 2, 3 * HEAD_SIZE)
     bf16, f32 = jnp.bfloat16, jnp.float32
     dma = pltpu.SemaphoreType.DMA
     anywhere = pl.BlockSpec(memory_space=pl.ANY)
@@ -782,22 +827,22 @@
             pltpu.VMEM((chunks, 2, slots, length, chunk_width), bf16),
             pltpu.VMEM((chunks, 2, slots, length, chunk_width), bf16),
             pltpu.VMEM((ranks, batches, 8, length), f32),
-            pltpu.VMEM((heads, batches, length, packed), bf16),
-            pltpu.VMEM((heads, batches, length, packed), bf16),
-            pltpu.VMEM((heads, batches, length, packed), bf16),
-            pltpu.VMEM((heads, batches, length, packed), bf16),
-            pltpu.VMEM((heads, batches, length, packed), bf16),
-            pltpu.VMEM((heads, 2, slots, length, packed), bf16),
+            pltpu.VMEM((pieces, batches, *packed), bf16),
+            pltpu.VMEM((pieces, batches, *packed), bf16),
+            pltpu.VMEM((pieces, batches, *packed), bf16),
+            pltpu.VMEM((pieces, batches, *packed), bf16),
+            pltpu.VMEM((pieces, batches, *packed), bf16),
+            pltpu.VMEM((pieces, 2, slots, *packed), bf16),
             pltpu.VMEM((batches, heads, length, width // heads), bf16),
         ]
-        + [pltpu.VMEM((2, slots, length, packed), bf16)] * heads
+        + [pltpu.VMEM((2, slots, *packed), bf16)] * pieces
         + [
             dma,
             dma,
             dma((chunks,)),
             dma((batches, heads)),
-            dma((batches,)),
-            dma((batches,)),
+            dma((4 * batches,)),
+            dma((4 * batches,)),
             dma,
             dma,
             dma,
@@ -808,12 +853,12 @@
             dma((chunks, 2)),
             dma((ranks - 1,)),
             dma((ranks - 1,)),
-            dma((heads,)),
-            dma((heads,)),
-            dma((heads,)),
-            dma((heads,)),
-            dma((heads, 2)),
-            dma((heads, 2)),
+            dma((pieces,)),
+            dma((pieces,)),
+            dma((pieces,)),
+            dma((pieces,)),
+            dma((pieces, 2)),
+            dma((pieces, 2)),
         ],
         compiler_params=pltpu.CompilerParams(
             collective_id=slots, has_side_effects=True, vmem_limit_bytes=62 * 2**20
@@ -832,13 +877,14 @@
 def fused_shards(tokens, queries, segment_ids, gain, key_value_weight, plan):
     ranks = lax.axis_size("dp")
     batches = segment_ids.shape[0]
-    target = plan // batches
-    source = jnp.arange(plan.shape[0], dtype=jnp.int32) // batches
-    cuts = jnp.arange(1, ranks, dtype=jnp.int32)[:, None]
-    crossing = jnp.sum((source < cuts) & (target >= cuts), axis=1)
     most = batches * (ranks // 2)
     branches = [functools.partial(fused, slots) for slots in range(batches, most + 1)]
-    index = jnp.clip(jnp.max(crossing) - batches, 0, most - batches)
+    source = np.arange(plan.shape[0]) // batches
+    crossing = [
+        jnp.sum(jnp.where(source < cut, plan >= cut * batches, False).astype(jnp.int32))
+        for cut in range(2, ranks - 1)
+    ]
+    index = jnp.clip(functools.reduce(jnp.maximum, crossing, batches) - batches, 0, most - batches)
     return lax.switch(
         index, branches, plan, tokens, queries, segment_ids, gain, key_value_weight
     )

time: 119 us -> 99.5 us (0.84); the launches traced: 117 us -> 99.2 us
  Pallas kernels: 112 us -> 93.9 us
    pallas_call x1, Pallas kernels: 112 us -> 93.9 us  [fused(): pl.pallas_call(functools.partial(fused_kernel, slots), out_shape=jax.Shap...]
where the time goes in v2:
time: 99.5 us; the launch traced here: 99.2 us
  Pallas kernels  93.9 us (94%)
  local copies, waits for them, and re-layouts  3.13 us (3%)
  other arithmetic  1.31 us (1%)
    pallas_call x1, Pallas kernels, fused(): pl.pallas_call(functools.partial(fused_kernel, slots), out_shape=jax.Shap...  93.9 us
    unnamed x1, local copies, waits for them, and re-layouts  3.13 us

profile of v2, /device:TPU:0, one launch (start us, length us, event | category | flops | bytes accessed | tf_op | source)
XLA Modules:
  0.0 99.2 jit_solution(15207066050481439902)
XLA Ops:
  0.0 1.3 %fusion = s32[]{:T(128)} fusion(pred[8]{0:T(512)(128)(4,1)} %constant.12.clone, s32[8]{0:T(128)} %param.15), kind=kLoop, calls=%fused_computation.1 | loop fusion | flops 31 | bytes 44 | tf_op jit(solution)/shard_map/reduce_sum | solution.py:884
  2.0 94.1 %conditional.1 = (bf16[256,4096]{1,0:T(8,128)(2,1)}) conditional(s32[]{:T(128)} %clamp.3, (bf16[256,4096]{1,0:T(8,128)(2,1)}, bf16[256,4096]{1,0:T(8,128)(2,1)}, f32[4096]{0:T(1024)}, s32[8]{0:T(128)}, s32[2,128]{1,0:T(2,128)}, /*index=5*/bf16[4096,512]{1,0:T(8,128)(2,1)}) %tuple.14, (bf16[256,4096]{1,0:T(8,128)(2,1)}, ...), branch_computations={%region_1.2_spmd, %region_2.3_spmd, %region_3.4_spmd} | conditional | bytes 8 | solution.py:888
  2.0 93.9 %fused.3 = bf16[256,4096]{1,0:T(8,128)(2,1)} custom-call(s32[8]{0:T(128)} %get-tuple-element.44.plan_ref, bf16[2,128,4096]{2,1,0:T(8,128)(2,1)} %bitcast.9, bf16[2,128,4096]{2,1,0:T(8,128)(2,1)} %bitcast.12, s32[2,128]{1,0:T(2,128)} %get-tuple-element.48.document_ref, f32[1,4096]{1,0:T(1,128)} %bitcast.15, bf16[4096,512]{1,0:T(8,128)(2,1)} %get-tuple-element.50.weight_ref), custom_call_target="tpu_custom_call" | custom-call | tf_op jit(solution)/shard_map/cond/branch_0_fun/fused/pallas_call | solution.py:806
  96.1 3.1 %copy.15 = bf16[256,4096]{1,0:T(8,128)(2,1)} copy(bf16[256,4096]{1,0:T(8,128)(2,1)} %get-tuple-element.63) | data formatting | bytes 4194304

commit v3 on v2

--- a/solution.py
+++ b/solution.py
@@ -295,7 +295,6 @@
     parts_b,
     kv_own,
     kv_out,
-    mixed,
     *rest,
 ):
     pieces = parts_a.shape[0]
@@ -304,8 +303,7 @@
         load_rows,
         load_weight,
         load_query,
-        store_out,
-        rows_send,
+            rows_send,
         rows_recv,
         weight_send,
         weight_recv,
@@ -327,7 +325,7 @@
     ranks = lax.axis_size("dp")
     me, f, t = lax.axis_index("dp"), lax.axis_index("fsdp"), lax.axis_index("tensor")
     batches, length, depth = own_rows.shape
-    heads = mixed.shape[1]
+    heads = weight.shape[2] // HEAD_SIZE
     height = parts_a.shape[2]
     per_piece = pieces // heads
     tall = length // 4
@@ -381,7 +379,7 @@
 
     rows_moves = []
     for q in range(strips):
-        part = (q * tall // length, pl.ds(q * tall % length, tall))
+        part = (q % batches, pl.ds(q // batches * tall, tall))
         rows_moves.append(
             remote(
                 tokens_ref.at[part],
@@ -428,6 +426,7 @@
     ]
     for move in document_moves:
         move.start()
+
 
     plan = [plan_ref[i] for i in range(ranks * batches)]
     routes = [route(plan, ranks, batches, slots, me, step) for step in (1, -1)]
@@ -537,14 +536,15 @@
         normalize(own_rows, scale_own, s, 0, length)
 
     def multiply(rows, h):
+        count = rows.shape[1]
         half = heads // 2
         start = pl.multiple_of((h % half) * 2 * HEAD_SIZE, 2 * HEAD_SIZE)
         part = jnp.dot(
-            rows[...].reshape(batches * length, depth),
+            rows.reshape(batches * count, depth),
             weight[h // half, :, pl.ds(start, 2 * HEAD_SIZE)],
             preferred_element_type=jnp.float32,
         )
-        return pack_parts(part).reshape(batches, length, 3 * HEAD_SIZE)
+        return pack_parts(part).reshape(batches, count, 3 * HEAD_SIZE)
 
     def own_copy(i):
         return remote(
@@ -562,9 +562,9 @@
         )
 
     def own_head(h):
-        packed = multiply(own_rows, h)
+        packed = multiply(own_rows[...], h)
         for j in range(per_piece):
-            i = h * per_piece + j
+            i = j * heads + h
             piece = packed[:, j * height : (j + 1) * height]
 
             @pl.when(off)
@@ -576,14 +576,9 @@
             def _():
                 parts_a[i] = piece
 
-    def far_head(h):
-        packed = multiply(far_rows, h)
-        for j in range(per_piece):
-            far_parts[h * per_piece + j] = packed[:, j * height : (j + 1) * height]
-
     def send_far(i):
-        if i % per_piece == 0:
-            far_head(i // per_piece)
+        top = i // heads * height
+        far_parts[i] = multiply(far_rows[:, top : top + height], i % heads)
 
         @pl.when(off)
         def _():
@@ -597,9 +592,9 @@
         rows_moves[q].wait_recv()
         if q == 0:
             scale_move.wait_recv()
-        normalize(far_rows, scale_far, q * tall // length, q * tall % length, tall)
-
-    taken = 0
+        normalize(far_rows, scale_far, q % batches, q // batches * tall, tall)
+
+    taken = early = 0
     later = list(range(chunks + 1))
     while taken < strips:
         c = later.pop(0)
@@ -616,6 +611,9 @@
         while taken < upto:
             take_rows(taken)
             taken += 1
+        if early < heads and taken * tall >= batches * height:
+            send_far(early)
+            early += 1
 
     def kv_copy(way, h):
         return remote(
@@ -680,14 +678,6 @@
         )
         return jnp.where(left_at >= 0, coming(1, jnp.maximum(left_at, 0)), value)
 
-    def out_copy(s, h):
-        wide = group * HEAD_SIZE
-        return pltpu.make_async_copy(
-            mixed.at[s, h],
-            out_ref.at[pl.ds(s * length, length), pl.ds(h * wide, wide)],
-            store_out.at[s, h],
-        )
-
     spots = [place_of(s) for s in range(batches)]
 
     def settle(copy, index):
@@ -698,7 +688,7 @@
                 copy(way, index).wait_recv()
 
     def attend_head(h):
-        for i in range(h * per_piece, (h + 1) * per_piece):
+        for i in range(h, pieces, heads):
             settle(kv_copy, i)
 
         @pl.loop(0, batches)
@@ -715,7 +705,7 @@
             kv = jnp.concatenate(
                 [
                     pick(lambda at: kv_own[i, at], lambda way, at: kv_in[i][way, at], places)
-                    for i in range(h * per_piece, (h + 1) * per_piece)
+                    for i in range(h, pieces, heads)
                 ],
                 axis=0,
             )
@@ -737,35 +727,41 @@
                 value,
                 preferred_element_type=jnp.float32,
             ).astype(jnp.bfloat16)
+            top = pl.multiple_of(s * length, length)
             for g in range(group):
-                mixed[s, h, :, g * HEAD_SIZE : (g + 1) * HEAD_SIZE] = result[
+                start = (h * group + g) * HEAD_SIZE
+                out_ref[pl.ds(top, length), start : start + HEAD_SIZE] = result[
                     g * length : (g + 1) * length
                 ]
-            out_copy(s, h).start()
-
-    for i in range(pieces):
+
+    def kv_round(i):
+        join(i)
+        kv_step(first, i)
+        if i == 1:
+            query_round(later.pop(0))
+        if i >= 2:
+            kv_step(second_way, i - 2)
+
+    rounds_done = 0
+    for i in range(early, pieces):
         send_far(i)
-        if i == per_piece - 1 and len(later) > 1:
+        if i >= heads and len(later) > 1:
             query_round(later.pop(0))
+        elif i > heads and len(later) <= 1:
+            kv_round(rounds_done)
+            rounds_done += 1
     while len(later) > 1:
         query_round(later.pop(0))
-    for step in range(pieces + 1):
-        if step < pieces:
-            join(step)
-            kv_step(first, step)
-        if step == 1:
-            query_round(later.pop(0))
-            for c in rounds:
-                settle(query_copy, c)
-            for move in document_arrivals:
-                move.wait_recv()
-        if step >= 2:
-            kv_step(second_way, step - 2)
-        if step == pieces:
-            kv_step(second_way, step - 1)
-        if step == pieces:
-            for h in range(heads):
-                attend_head(h)
+    for i in range(rounds_done, pieces):
+        kv_round(i)
+    for i in range(pieces - 2, pieces):
+        kv_step(second_way, i)
+    for c in rounds:
+        settle(query_copy, c)
+    for move in document_arrivals:
+        move.wait_recv()
+    for h in range(heads):
+        attend_head(h)
 
     for move in rows_moves + [weight_move, stats_move, scale_move] + document_moves:
         move.wait_send()
@@ -785,9 +781,6 @@
             own_copy(i).wait_send()
 
         far_copy_a(i).wait_send()
-    for h in range(heads):
-        for s in range(batches):
-            out_copy(s, h).wait()
 
 
 def fused(slots, plan, tokens, queries, segment_ids, gain, key_value_weight):
@@ -796,11 +789,12 @@
     rows, depth = tokens.shape
     width = queries.shape[1]
     heads = 2 * key_value_weight.shape[1] // (2 * HEAD_SIZE)
-    chunks = 2 * heads
+    chunks = 4 * heads
     chunk_width = width // chunks
     pieces = 2 * heads
     packed = (length // 2, 3 * HEAD_SIZE)
     bf16, f32 = jnp.bfloat16, jnp.float32
+    limit = (5 + slots) * 6 * 2**20
     dma = pltpu.SemaphoreType.DMA
     anywhere = pl.BlockSpec(memory_space=pl.ANY)
     return pl.pallas_call(
@@ -814,7 +808,7 @@
             pl.BlockSpec(memory_space=pltpu.VMEM),
             anywhere,
         ],
-        out_specs=anywhere,
+        out_specs=pl.BlockSpec(memory_space=pltpu.VMEM),
         scratch_shapes=[
             pltpu.VMEM((batches, length, depth), bf16),
             pltpu.VMEM((batches, length, depth), bf16),
@@ -833,14 +827,12 @@
             pltpu.VMEM((pieces, batches, *packed), bf16),
             pltpu.VMEM((pieces, batches, *packed), bf16),
             pltpu.VMEM((pieces, 2, slots, *packed), bf16),
-            pltpu.VMEM((batches, heads, length, width // heads), bf16),
         ]
         + [pltpu.VMEM((2, slots, *packed), bf16)] * pieces
         + [
             dma,
             dma,
             dma((chunks,)),
-            dma((batches, heads)),
             dma((4 * batches,)),
             dma((4 * batches,)),
             dma,
@@ -861,7 +853,7 @@
             dma((pieces, 2)),
         ],
         compiler_params=pltpu.CompilerParams(
-            collective_id=slots, has_side_effects=True, vmem_limit_bytes=62 * 2**20
+            collective_id=slots, has_side_effects=True, vmem_limit_bytes=limit
         ),
         name="fused",
     )(

time: 99.5 us -> 90.2 us (0.907)
  Pallas kernels: 93.9 us -> 86.4 us
  local copies, waits for them, and re-layouts: 3.13 us -> 1.32 us
    pallas_call x1, Pallas kernels: 93.9 us -> 86.4 us  [fused(): pl.pallas_call(functools.partial(fused_kernel, slots), out_shape=jax.Shap...]
    unnamed x1, local copies, waits for them, and re-layouts: 3.13 us -> 1.32 us
where the time goes in v3:
time: 90.2 us; the launch traced here: 89.9 us
  Pallas kernels  86.4 us (96%)
  local copies, waits for them, and re-layouts  1.32 us (1%)
  other arithmetic  1.31 us (1%)
    pallas_call x1, Pallas kernels, fused(): pl.pallas_call(functools.partial(fused_kernel, slots), out_shape=jax.Shap...  86.4 us

profile of v3, /device:TPU:0, one launch (start us, length us, event | category | flops | bytes accessed | tf_op | source)
XLA Modules:
  0.0 89.9 jit_solution(11182542004717567067)
XLA Ops:
  0.0 1.3 %fusion = s32[]{:T(128)} fusion(pred[8]{0:T(512)(128)(4,1)} %constant.12.clone, s32[8]{0:T(128)} %param.15), kind=kLoop, calls=%fused_computation.1 | loop fusion | flops 31 | bytes 44 | tf_op jit(solution)/shard_map/reduce_sum | solution.py:876
  2.0 86.6 %conditional.1 = (bf16[256,4096]{1,0:T(8,128)(2,1)S(1)}) conditional(s32[]{:T(128)} %clamp.3, (bf16[256,4096]{1,0:T(8,128)(2,1)}, bf16[256,4096]{1,0:T(8,128)(2,1)}, f32[4096]{0:T(1024)}, s32[8]{0:T(128)}, s32[2,128]{1,0:T(2,128)}, /*index=5*/bf16[4096,512]{1,0:T(8,128)(2,1)}) %tuple.14, (bf16[256,4096]{1,0:T(8,128)(2,1)}, ...), branch_computations={%region_1.2_spmd, %region_2.3_spmd, %region_3.4_spmd} | conditional | bytes 8 | solution.py:880
  2.0 86.4 %fused.3 = bf16[256,4096]{1,0:T(8,128)(2,1)S(1)} custom-call(s32[8]{0:T(128)} %get-tuple-element.44.plan_ref, bf16[2,128,4096]{2,1,0:T(8,128)(2,1)} %bitcast.9, bf16[2,128,4096]{2,1,0:T(8,128)(2,1)} %bitcast.12, s32[2,128]{1,0:T(2,128)} %get-tuple-element.48.document_ref, f32[1,4096]{1,0:T(1,128)} %bitcast.15, bf16[4096,512]{1,0:T(8,128)(2,1)} %get-tuple-element.50.weight_ref), custom_call_target="tpu_custom_call" | custom-call | tf_op jit(solution)/shard_map/cond/branch_0_fun/fused/pallas_call | solution.py:800
  88.6 1.3 %copy.15 = bf16[256,4096]{1,0:T(8,128)(2,1)} copy(bf16[256,4096]{1,0:T(8,128)(2,1)S(1)} %get-tuple-element.63) | data formatting | bytes 4194304
